TPU v7x, 32 devices: a whole 2x2x4 slice. The times are simulated.
32 devices in a mesh: lon: 8 (over y, x, core), dp: 4 (over z).
Axes of the slice: x: 2, y: 2, z: 4, core: 2. Of those that a mesh axis runs over, the one named last changes fastest.
Arguments:
- inputs: bfloat16 [4, 32, 384, 256], P('dp', None, 'lon'), may hold values from -6 to 6
- pre_act: bfloat16 [4, 32, 384, 256], P('dp', None, 'lon'), may hold values from -6 to 6
- cotangent: bfloat16 [4, 32, 384, 256], P('dp', None, 'lon'), may hold values from -6 to 6
- first_weight: bfloat16 [2304, 256], replicated, may hold values from -0.125 to 0.125
- second_weight: bfloat16 [2304, 256], replicated, may hold values from -0.125 to 0.125
Outputs:
- input_gradient_array: bfloat16 [4, 32, 384, 256], P('dp', None, 'lon')
- first_weight_gradient: float32 [589824], P(('lon', 'dp'))
- second_weight_gradient: float32 [589824], P(('lon', 'dp'))
All inputs are finite; a program needn't handle non-finite values.
Results may differ from a plain program's by a relative error of at most 0.0049.
Values may be sent and summed in bfloat16 or wider, within the bound.
No kernel may reach another device: no remote copies, remote signals or barrier semaphores. Data moves between devices by JAX's collectives and lax.ppermute only.
A program may use at most 64 MiB of HBM per device.

v0:
```python
import functools

import jax
import jax.numpy as jnp
from jax import lax
from jax.experimental import pallas as pl
from jax.experimental.pallas import tpu as pltpu
from jax.sharding import PartitionSpec as P


FIRST_SPREAD = 12
SECOND_SPREAD = 18
FIRST_PAD = 4
SECOND_PAD = 2
BF16 = jnp.bfloat16
F32 = jnp.float32


def moved_rows(row, low, high, spread):
    cols = row.shape[0]
    return (
        jnp.concatenate([row[spread:], high], axis=0).astype(BF16),
        jnp.concatenate([low, row[: cols - spread]], axis=0).astype(BF16),
    )


def build_views(src, low, high, views, spread, pad, plus, minus):
    rows, cols, chans = src.shape
    if pad:
        blank = jnp.zeros((pad * cols, 3 * chans), BF16)
        views[: pad * cols, :] = blank
        views[(pad + rows) * cols :, :] = blank
    for p in range(rows):
        at = pl.ds((pad + p) * cols, cols)
        row = src[p]
        views[at, chans : 2 * chans] = row
        row = row.astype(F32)
        if low is None:
            upper = lower = jnp.zeros((spread, chans), F32)
        else:
            strip = pl.ds(p * spread, spread)
            upper = high[strip, :].astype(F32)
            lower = low[strip, :].astype(F32)
        ahead, behind = moved_rows(row, lower, upper, spread)
        views[at, plus * chans : (plus + 1) * chans] = ahead
        views[at, minus * chans : (minus + 1) * chans] = behind


def transpose_taps(weight, turned):
    chans = weight.shape[1]
    for k in range(9):
        turned[k * chans : (k + 1) * chans, :] = weight[k * chans : (k + 1) * chans, :].T


def input_side(views, turned, total, rows, cols, spread, pad):
    part = (rows - spread) * cols
    first = pad * cols
    third = turned.shape[0] // 3
    total[...] = jnp.dot(
        views[first : first + rows * cols, :],
        turned[third : 2 * third, :],
        preferred_element_type=F32,
    )
    ahead = (pad + spread) * cols
    total[:part, :] += jnp.dot(
        views[ahead : ahead + part, :], turned[:third, :], preferred_element_type=F32
    )
    total[spread * cols :, :] += jnp.dot(
        views[first : first + part, :], turned[2 * third :, :], preferred_element_type=F32
    )


def tap_rows(rows, cols, spread, pad, direction):
    block = rows - spread + pad
    ahead = (0, block * cols, (pad + spread) * cols)
    middle = (0, rows * cols, pad * cols)
    behind = ((rows - block) * cols, rows * cols, 0)
    return (ahead, middle, behind) if direction < 0 else (behind, middle, ahead)


def product(still, views, span):
    low, high, start = span
    return jnp.dot(
        still[:, low:high], views[start : start + high - low, :], preferred_element_type=F32
    )


def place_tap(gradient, k, block):
    chans = block.shape[0]
    half = chans // 2
    for h in range(2):
        at = pl.ds(2 * k * chans + h, chans, stride=2)
        gradient[at, :] = block[:, h * half : (h + 1) * half]


def hand_out(gradient, keep, send, segments):
    size = gradient.shape[0] // segments
    place = lax.axis_index("lon")
    core = lax.rem(place, 2)
    chip = place // 2
    for m in range(segments // 2):
        pair = 2 * lax.bitwise_xor(chip, m)
        mine = pl.ds(pl.multiple_of((pair + core) * size, size), size)
        other = pl.ds(pl.multiple_of((pair + 1 - core) * size, size), size)
        keep[m * size : (m + 1) * size, :] = gradient[mine, :].astype(BF16)
        send[m * size : (m + 1) * size, :] = gradient[other, :].astype(BF16)


def second_early_kernel(pre, cot, weight, total, taps, low_still, high_still, turned, views, still):
    rows, cols, chans = pre.shape
    spread, pad = SECOND_SPREAD, SECOND_PAD
    build_views(cot, None, None, views, spread, pad, 0, 2)
    transpose_taps(weight, turned)
    hidden = pre[...]
    hidden = jnp.maximum(hidden, jnp.zeros_like(hidden))
    still[...] = hidden.reshape(rows * cols, chans).T
    half = cols // 2
    low_still[...] = hidden[:, :half].reshape(rows * half, chans).T
    high_still[...] = hidden[:, half:].reshape(rows * half, chans).T
    input_side(views, turned, total, rows, cols, spread, pad)
    for r, span in enumerate(tap_rows(rows, cols, spread, pad, -1)):
        value = product(still, views, span)
        for c in range(3):
            k = 3 * r + c
            taps[k * chans : (k + 1) * chans, :] = value[:, c * chans : (c + 1) * chans]


def second_late_kernel(
    norm, segments, pre, low, high, early, taps, low_still, high_still, turned,
    keep, send, local, edge_low, edge_high, low_views, high_views, low_total, high_total, gradient,
):
    rows, cols, chans = pre.shape
    spread, pad = SECOND_SPREAD, SECOND_PAD
    half = cols // 2
    blank = jnp.zeros((pad * half, chans), BF16)
    for views in (low_views, high_views):
        views[: pad * half, :] = blank
        views[(pad + rows) * half :, :] = blank
    gap = jnp.zeros((half - spread, chans), F32)
    for p in range(0, rows, 2):
        at = pl.ds((pad + p) * half, 2 * half)
        lower = [low[q * spread : (q + 1) * spread, :].astype(F32) for q in (p, p + 1)]
        upper = [high[q * spread : (q + 1) * spread, :].astype(F32) for q in (p, p + 1)]
        low_views[at, :] = jnp.concatenate([lower[0], gap, lower[1], gap], axis=0).astype(BF16)
        high_views[at, :] = jnp.concatenate([gap, upper[0], gap, upper[1]], axis=0).astype(BF16)

    part = (rows - spread) * half
    first = pad * half
    ahead = (pad + spread) * half
    for views, total, c in ((low_views, low_total, 2), (high_views, high_total, 0)):

        def matrix(r):
            k = 3 * r + c
            return turned[k * chans : (k + 1) * chans, :]

        total[...] = jnp.dot(
            views[first : first + rows * half, :], matrix(1), preferred_element_type=F32
        )
        total[:part, :] += jnp.dot(
            views[ahead : ahead + part, :], matrix(0), preferred_element_type=F32
        )
        total[spread * half :, :] += jnp.dot(
            views[first : first + part, :], matrix(2), preferred_element_type=F32
        )
    width = FIRST_SPREAD
    for p in range(rows):
        at = pl.ds(p * half, half)
        value = early[p * cols : (p + 1) * cols, :] + jnp.concatenate(
            [low_total[at, :], high_total[at, :]], axis=0
        )
        value = jnp.where(pre[p].astype(F32) > 0, value, jnp.float32(0.0))
        local[p] = value.astype(BF16)
        edge_low[p * width : (p + 1) * width, :] = value[:width].astype(BF16)
        edge_high[p * width : (p + 1) * width, :] = value[cols - width :].astype(BF16)
    for r, span in enumerate(tap_rows(rows, half, spread, pad, -1)):
        side = {0: product(high_still, high_views, span), 2: product(low_still, low_views, span)}
        for c in range(3):
            k = 3 * r + c
            block = taps[k * chans : (k + 1) * chans, :]
            if c in side:
                block = block + side[c]
            place_tap(gradient, k, norm * block)
    hand_out(gradient, keep, send, segments)


def first_weight_kernel(
    norm, segments, inputs, low, high, local, keep, send, views, still, gradient
):
    rows, cols, chans = inputs.shape
    spread, pad = FIRST_SPREAD, FIRST_PAD
    build_views(inputs, low, high, views, spread, pad, 2, 0)
    still[...] = local[...].reshape(rows * cols, chans).T
    for r, span in enumerate(tap_rows(rows, cols, spread, pad, 1)):
        value = (norm * product(still, views, span)).astype(BF16)
        for c in range(3):
            block = value[:, c * chans : (c + 1) * chans].T
            place_tap(gradient, 3 * r + c, block.astype(F32))
    hand_out(gradient, keep, send, segments)


def first_input_kernel(local, low, high, weight, out, views, turned, total):
    rows, cols, chans = local.shape
    build_views(local, low, high, views, FIRST_SPREAD, 0, 0, 2)
    transpose_taps(weight, turned)
    input_side(views, turned, total, rows, cols, FIRST_SPREAD, 0)
    out[...] = total[...].astype(BF16).reshape(rows, cols, chans)


def edges_kernel(width, field, low, high):
    rows, cols, _ = field.shape
    for p in range(rows):
        row = field[p]
        low[p * width : (p + 1) * width, :] = row[:width]
        high[p * width : (p + 1) * width, :] = row[cols - width :]


def pair_kernel(keep, received, *outs):
    size = outs[0].shape[0]
    for m, out in enumerate(outs):
        at = pl.ds(m * size, size)
        out[...] = (keep[at, :].astype(F32) + received[at, :].astype(F32)).astype(BF16)


def chip_kernel(count, *refs):
    terms, own, pieces, level = refs[:count], refs[count], refs[count + 1 : -1], refs[-1]
    level[...] = sum((t[...].astype(F32) for t in terms[1:]), terms[0][...].astype(F32))
    size = own.shape[0]
    me = lax.axis_index("dp")

    def piece(m):
        start = pl.multiple_of(lax.bitwise_xor(me, m) * size, size)
        return level[pl.ds(start, size), :]

    own[...] = piece(0)
    for m, out in enumerate(pieces):
        out[...] = piece(m + 1).astype(BF16)


def last_kernel(own, *refs):
    refs[-1][...] = sum((t[...].astype(F32) for t in refs[:-1]), own[...])


def call(kernel, outs, scratch, *operands, limit=20, flops=0):
    whole = pl.BlockSpec(memory_space=pltpu.VMEM)
    return pl.pallas_call(
        kernel,
        out_shape=[jax.ShapeDtypeStruct(s, t) for s, t in outs],
        in_specs=[whole] * len(operands),
        out_specs=[whole] * len(outs),
        scratch_shapes=[pltpu.VMEM(s, t) for s, t in scratch],
        compiler_params=pltpu.CompilerParams(vmem_limit_bytes=limit * 2**20),
    )(*operands)


def ring(axis, step):
    count = lax.axis_size(axis)
    return [(i, (i + step) % count) for i in range(count)]


def swap(axis, mask):
    return [(i, i ^ mask) for i in range(lax.axis_size(axis))]


def exchange_edges(low_edge, high_edge):
    low = lax.ppermute(high_edge, "lon", ring("lon", 1))
    high = lax.ppermute(low_edge, "lon", ring("lon", -1))
    return low, high


def edges_of(field, width):
    shape = (field.shape[0] * width, field.shape[2])
    return call(functools.partial(edges_kernel, width), [(shape, BF16)] * 2, [], field, limit=4)


def reduce_partials(keep, send):
    chips = lax.axis_size("lon") // 2
    parts = lax.axis_size("dp")
    rows, lanes = keep.shape
    received = lax.ppermute(send, "lon", swap("lon", 1))
    piece = (rows // chips, lanes)
    paired = call(pair_kernel, [(piece, BF16)] * chips, [], keep, received, limit=4)
    arrived = [lax.ppermute(paired[m], "lon", swap("lon", 2 * m)) for m in range(1, chips)]
    small = (piece[0] // parts, lanes)
    own, *pieces = call(
        functools.partial(chip_kernel, chips),
        [(small, F32)] + [(small, BF16)] * (parts - 1),
        [(piece, F32)],
        paired[0], *arrived, limit=4,
    )
    arrived = [lax.ppermute(pieces[m - 1], "dp", swap("dp", m)) for m in range(1, parts)]
    (total,) = call(last_kernel, [(small, F32)], [], own, *arrived, limit=4)
    return total.reshape(-1)


def local(inputs, pre_act, cotangent, first_weight, second_weight):
    shape = inputs.shape
    inputs, pre_act, cotangent = (a.reshape(a.shape[1:]) for a in (inputs, pre_act, cotangent))
    rows, cols, chans = inputs.shape
    segments = lax.axis_size("lon")
    cells = rows * cols
    norm = float(shape[0] * cells * segments * lax.axis_size("dp")) ** -0.5
    taps = first_weight.shape[0]
    cot_low, cot_high = exchange_edges(*edges_of(cotangent, SECOND_SPREAD))
    in_low, in_high = exchange_edges(*edges_of(inputs, FIRST_SPREAD))
    matrix = (taps, chans)
    pieces = (taps, chans // 2)
    grid = (2 * taps, chans // 2)
    edge = (rows * FIRST_SPREAD, chans)
    side = (cells // 2, chans)
    early = call(
        second_early_kernel,
        [
            ((cells, chans), F32),
            (matrix, F32),
            (side[::-1], BF16),
            (side[::-1], BF16),
            (matrix, BF16),
        ],
        [(((rows + 2 * SECOND_PAD) * cols, 3 * chans), BF16), ((chans, cells), BF16)],
        pre_act, cotangent, second_weight,
    )
    strip = ((rows + 2 * SECOND_PAD) * cols // 2, chans)
    keep, send, local_grad, edge_low, edge_high = call(
        functools.partial(second_late_kernel, norm, segments),
        [(pieces, BF16), (pieces, BF16), ((rows, cols, chans), BF16), (edge, BF16), (edge, BF16)],
        [(strip, BF16), (strip, BF16), (side, F32), (side, F32), (grid, F32)],
        pre_act, cot_low, cot_high, *early,
    )
    second = reduce_partials(keep, send)
    keep, send = call(
        functools.partial(first_weight_kernel, norm, segments),
        [(pieces, BF16), (pieces, BF16)],
        [
            (((rows + 2 * FIRST_PAD) * cols, 3 * chans), BF16),
            ((chans, cells), BF16),
            (grid, F32),
        ],
        inputs, in_low, in_high, local_grad,
    )
    first = reduce_partials(keep, send)
    grad_low, grad_high = exchange_edges(edge_low, edge_high)
    (input_gradient,) = call(
        first_input_kernel,
        [((rows, cols, chans), BF16)],
        [((cells, 3 * chans), BF16), (matrix, BF16), ((cells, chans), F32)],
        local_grad, grad_low, grad_high, first_weight,
    )
    return input_gradient.reshape(shape), first, second


def solution(mesh):
    field = P("dp", None, "lon", None)
    return jax.shard_map(
        local,
        mesh=mesh,
        in_specs=(field, field, field, P(), P()),
        out_specs=(field, P(("lon", "dp")), P(("lon", "dp"))),
        check_vma=False,
    )
```

profile of v0, /device:TPU:0, one launch (start us, length us, event | category | flops | bytes accessed | tf_op | source)
XLA Modules:
  0.0 52.4 jit_solution(15620451693614810746)
XLA Ops:
  0.7 1.2 %copy-done.1 = bf16[1,32,48,256]{3,2,1,0:T(8,128)(2,1)S(1)} copy-done((bf16[1,32,48,256]{3,2,1,0:T(8,128)(2,1)S(1)}, bf16[1,32,48,256]{3,2,1,0:T(8,128)(2,1)}, u32[]{:S(2)}) %copy-start.1) | copy-done | bytes 786456
  1.8 0.1 shard_map.76
  1.9 0.5 %collective-permute-start = (bf16[576,256]{1,0:T(8,128)(2,1)S(1)}, bf16[576,256]{1,0:T(8,128)(2,1)S(1)}, u32[]{:S(2)}, u32[]{:S(2)}) collective-permute-start(bf16[576,256]{1,0:T(8,128)(2,1)S(1)} %get-tuple-element.35), channel_id=1, source_target_pairs={{0,4},{4,8},{8,12},{12,16},{16,20},{20,24},{24,28},{28,0},{1,5},{5... | collective-permute-start | bytes 884744 | tf_op jit(solution)/shard_map/ppermute | solution.py:265
  2.5 2.9 %collective-permute-start.1 = (bf16[576,256]{1,0:T(8,128)(2,1)S(1)}, bf16[576,256]{1,0:T(8,128)(2,1)S(1)}, u32[]{:S(2)}, u32[]{:S(2)}) collective-permute-start(bf16[576,256]{1,0:T(8,128)(2,1)S(1)} %get-tuple-element.36), channel_id=1, source_target_pairs={{0,28},{4,0},{8,4},{12,8},{16,12},{20,16},{24,20},{28,24},{1,29},{... | collective-permute-start | bytes 884744 | tf_op jit(solution)/shard_map/ppermute | solution.py:266
  5.4 1.1 %copy-done.3 = bf16[1,32,48,256]{3,2,1,0:T(8,128)(2,1)S(1)} copy-done((bf16[1,32,48,256]{3,2,1,0:T(8,128)(2,1)S(1)}, bf16[1,32,48,256]{3,2,1,0:T(8,128)(2,1)}, u32[]{:S(2)}) %copy-start.3) | copy-done | bytes 786456
  6.6 0.1 collective-permute-start.4
  6.6 2.6 %collective-permute-start.5 = (bf16[384,256]{1,0:T(8,128)(2,1)S(1)}, bf16[384,256]{1,0:T(8,128)(2,1)S(1)}, u32[]{:S(2)}, u32[]{:S(2)}) collective-permute-start(bf16[384,256]{1,0:T(8,128)(2,1)S(1)} %get-tuple-element.46), channel_id=1, source_target_pairs={{0,28},{4,0},{8,4},{12,8},{16,12},{20,16},{24,20},{28,24},{1,29},{... | collective-permute-start | bytes 589832 | tf_op jit(solution)/shard_map/ppermute | solution.py:266
  9.3 1.3 %copy-done.6 = bf16[2304,256]{1,0:T(8,128)(2,1)S(1)} copy-done((bf16[2304,256]{1,0:T(8,128)(2,1)S(1)}, bf16[2304,256]{1,0:T(8,128)(2,1)}, u32[]{:S(2)}) %copy-start.6) | copy-done | bytes 1179672
  10.6 2.6 %shard_map.77 = (f32[1536,256]{1,0:T(8,128)S(1)}, f32[2304,256]{1,0:T(8,128)S(1)}, bf16[256,768]{1,0:T(8,128)(2,1)S(1)}, bf16[256,768]{1,0:T(8,128)(2,1)S(1)}, bf16[2304,256]{1,0:T(8,128)(2,1)S(1)}) custom-call(bf16[32,48,256]{2,1,0:T(8,128)(2,1)S(1)} %bitcast.6, bf16[32,48,256]{2,1,0:T(8,128)(2,1)S(1)} %bitcast.9, bf16[2304,256]{1,0:T(8,128)(2,1)S(1)} %copy-done.6), custom_call_target="tpu_custom_call" | custom-call | tf_op jit(solution)/shard_map/pallas_call | solution.py:245
  13.2 0.0 collective-permute-done.low
  13.2 0.0 collective-permute-done.1.high
  13.2 0.0 copy-start.4
  13.2 1.3 %shard_map.78 = (bf16[2304,128]{1,0:T(8,128)(2,1)S(1)}, bf16[2304,128]{1,0:T(8,128)(2,1)S(1)}, bf16[32,48,256]{2,1,0:T(8,128)(2,1)S(1)}, bf16[384,256]{1,0:T(8,128)(2,1)S(1)}, bf16[384,256]{1,0:T(8,128)(2,1)S(1)}) custom-call(bf16[32,48,256]{2,1,0:T(8,128)(2,1)S(1)} %bitcast.7, bf16[576,256]{1,0:T(8,128)(2,1)S(1)} %collective-permute-done.low, ...), custom_call_target="tpu_custom_call" | custom-call | tf_op jit(solution)/shard_map/pallas_call | solution.py:245
  14.5 1.5 %collective-permute-start.13 = (bf16[2304,128]{1,0:T(8,128)(2,1)S(1)}, bf16[2304,128]{1,0:T(8,128)(2,1)S(1)}, u32[]{:S(2)}, u32[]{:S(2)}) collective-permute-start(bf16[2304,128]{1,0:T(8,128)(2,1)S(1)} %get-tuple-element.58), channel_id=1, source_target_pairs={{0,4},{4,0},{8,12},{12,8},{16,20},{20,16},{24,28},{28,24},{1,5},{5... | collective-permute-start | bytes 1769480 | tf_op jit(solution)/shard_map/ppermute | solution.py:279
  16.0 0.0 collective-permute-done.4.low
  16.0 2.1 %shard_map.81 = (bf16[2304,128]{1,0:T(8,128)(2,1)S(1)}, bf16[2304,128]{1,0:T(8,128)(2,1)S(1)}) custom-call(bf16[32,48,256]{2,1,0:T(8,128)(2,1)S(1)} %bitcast.11, bf16[384,256]{1,0:T(8,128)(2,1)S(1)} %collective-permute-done.4.low, bf16[384,256]{1,0:T(8,128)(2,1)S(1)} %collective-permute-done.5.high, bf16[32,48,256]{2,1,0:T(8,128)(2,1)S(1)} %get-tuple-element.42.local), custom_call_target="tpu_custom_call" | custom-call | tf_op jit(solution)/shard_map/pallas_call | solution.py:245
  18.1 1.8 %collective-permute-start.6 = (bf16[2304,128]{1,0:T(8,128)(2,1)S(1)}, bf16[2304,128]{1,0:T(8,128)(2,1)S(1)}, u32[]{:S(2)}, u32[]{:S(2)}) collective-permute-start(bf16[2304,128]{1,0:T(8,128)(2,1)S(1)} %get-tuple-element.48), channel_id=1, source_target_pairs={{0,4},{4,0},{8,12},{12,8},{16,20},{20,16},{24,28},{28,24},{1,5},{5... | collective-permute-start | bytes 1769480 | tf_op jit(solution)/shard_map/ppermute | solution.py:279
  19.9 0.0 collective-permute-done.13.received
  19.9 0.1 shard_map.85
  20.1 1.6 %collective-permute-start.14 = (bf16[576,128]{1,0:T(8,128)(2,1)S(1)}, bf16[576,128]{1,0:T(8,128)(2,1)S(1)}, u32[]{:S(2)}, u32[]{:S(2)}) collective-permute-start(bf16[576,128]{1,0:T(8,128)(2,1)S(1)} %get-tuple-element.60), channel_id=1, source_target_pairs={{0,8},{4,12},{8,0},{12,4},{16,24},{20,28},{24,16},{28,20},{1,9},{5... | collective-permute-start | bytes 442376 | tf_op jit(solution)/shard_map/ppermute | solution.py:282
  21.6 0.5 collective-permute-start.15
  22.1 1.5 %collective-permute-start.16 = (bf16[576,128]{1,0:T(8,128)(2,1)S(1)}, bf16[576,128]{1,0:T(8,128)(2,1)S(1)}, u32[]{:S(2)}, u32[]{:S(2)}) collective-permute-start(bf16[576,128]{1,0:T(8,128)(2,1)S(1)} %get-tuple-element.62), channel_id=1, source_target_pairs={{0,24},{4,28},{8,16},{12,20},{16,8},{20,12},{24,0},{28,4},{1,25},{... | collective-permute-start | bytes 442376 | tf_op jit(solution)/shard_map/ppermute | solution.py:282
  23.6 0.0 collective-permute-done.6.received
  23.6 2.6 %collective-permute-start.3 = (bf16[384,256]{1,0:T(8,128)(2,1)S(1)}, bf16[384,256]{1,0:T(8,128)(2,1)S(1)}, u32[]{:S(2)}, u32[]{:S(2)}) collective-permute-start(bf16[384,256]{1,0:T(8,128)(2,1)S(1)} %get-tuple-element.44), channel_id=1, source_target_pairs={{0,28},{4,0},{8,4},{12,8},{16,12},{20,16},{24,20},{28,24},{1,29},{... | collective-permute-start | bytes 589832 | tf_op jit(solution)/shard_map/ppermute | solution.py:266
  26.3 0.1 shard_map.82
  26.4 0.3 collective-permute-done.14.refs_1_
  26.7 1.7 %collective-permute-start.7 = (bf16[576,128]{1,0:T(8,128)(2,1)S(1)}, bf16[576,128]{1,0:T(8,128)(2,1)S(1)}, u32[]{:S(2)}, u32[]{:S(2)}) collective-permute-start(bf16[576,128]{1,0:T(8,128)(2,1)S(1)} %get-tuple-element.50), channel_id=1, source_target_pairs={{0,8},{4,12},{8,0},{12,4},{16,24},{20,28},{24,16},{28,20},{1,9},{5... | collective-permute-start | bytes 442376 | tf_op jit(solution)/shard_map/ppermute | solution.py:282
  28.3 3.6 %collective-permute-done.15.refs_2_ = bf16[576,128]{1,0:T(8,128)(2,1)S(1)} collective-permute-done((bf16[576,128]{1,0:T(8,128)(2,1)S(1)}, bf16[576,128]{1,0:T(8,128)(2,1)S(1)}, u32[]{:S(2)}, u32[]{:S(2)}) %collective-permute-start.15) | collective-permute-done | bytes 147488 | tf_op jit(solution)/shard_map/ppermute | solution.py:282
  31.9 0.1 collective-permute-start.8
  32.1 0.0 collective-permute-done.16.refs_3_
  32.1 0.4 collective-permute-start.9
  32.4 0.1 shard_map.86
  32.5 4.7 %collective-permute-done.7.refs_1_ = bf16[576,128]{1,0:T(8,128)(2,1)S(1)} collective-permute-done((bf16[576,128]{1,0:T(8,128)(2,1)S(1)}, bf16[576,128]{1,0:T(8,128)(2,1)S(1)}, u32[]{:S(2)}, u32[]{:S(2)}) %collective-permute-start.7) | collective-permute-done | bytes 147488 | tf_op jit(solution)/shard_map/ppermute | solution.py:282
  37.2 1.6 %collective-permute-start.17 = (bf16[144,128]{1,0:T(8,128)(2,1)S(1)}, bf16[144,128]{1,0:T(8,128)(2,1)S(1)}, u32[]{:S(2)}, u32[]{:S(2)}) collective-permute-start(bf16[144,128]{1,0:T(8,128)(2,1)S(1)} %get-tuple-element.64), channel_id=1, source_target_pairs={{0,1},{1,0},{2,3},{3,2},{4,5},{5,4},{6,7},{7,6},{8,9},{9,8},{10,11... | collective-permute-start | bytes 110600 | tf_op jit(solution)/shard_map/ppermute | solution.py:290
  38.8 2.6 %collective-permute-start.18 = (bf16[144,128]{1,0:T(8,128)(2,1)S(1)}, bf16[144,128]{1,0:T(8,128)(2,1)S(1)}, u32[]{:S(2)}, u32[]{:S(2)}) collective-permute-start(bf16[144,128]{1,0:T(8,128)(2,1)S(1)} %get-tuple-element.65), channel_id=1, source_target_pairs={{0,2},{1,3},{2,0},{3,1},{4,6},{5,7},{6,4},{7,5},{8,10},{9,11},{10,... | collective-permute-start | bytes 110600 | tf_op jit(solution)/shard_map/ppermute | solution.py:290
  41.4 2.6 %collective-permute-start.19 = (bf16[144,128]{1,0:T(8,128)(2,1)S(1)}, bf16[144,128]{1,0:T(8,128)(2,1)S(1)}, u32[]{:S(2)}, u32[]{:S(2)}) collective-permute-start(bf16[144,128]{1,0:T(8,128)(2,1)S(1)} %get-tuple-element.66), channel_id=1, source_target_pairs={{0,3},{1,2},{2,1},{3,0},{4,7},{5,6},{6,5},{7,4},{8,11},{9,10},{10,... | collective-permute-start | bytes 110600 | tf_op jit(solution)/shard_map/ppermute | solution.py:290
  44.0 0.1 shard_map.83
  44.1 0.0 collective-permute-done.2.low
  44.1 0.1 collective-permute-start.10
  44.2 1.8 %collective-permute-start.11 = (bf16[144,128]{1,0:T(8,128)(2,1)S(1)}, bf16[144,128]{1,0:T(8,128)(2,1)S(1)}, u32[]{:S(2)}, u32[]{:S(2)}) collective-permute-start(bf16[144,128]{1,0:T(8,128)(2,1)S(1)} %get-tuple-element.55), channel_id=1, source_target_pairs={{0,2},{1,3},{2,0},{3,1},{4,6},{5,7},{6,4},{7,5},{8,10},{9,11},{10,... | collective-permute-start | bytes 110600 | tf_op jit(solution)/shard_map/ppermute | solution.py:290
  46.0 0.0 collective-permute-done.17.refs_0_
  46.0 2.6 %collective-permute-start.12 = (bf16[144,128]{1,0:T(8,128)(2,1)S(1)}, bf16[144,128]{1,0:T(8,128)(2,1)S(1)}, u32[]{:S(2)}, u32[]{:S(2)}) collective-permute-start(bf16[144,128]{1,0:T(8,128)(2,1)S(1)} %get-tuple-element.56), channel_id=1, source_target_pairs={{0,3},{1,2},{2,1},{3,0},{4,7},{5,6},{6,5},{7,4},{8,11},{9,10},{10,... | collective-permute-start | bytes 110600 | tf_op jit(solution)/shard_map/ppermute | solution.py:290
  48.6 2.5 %shard_map.79 = bf16[32,48,256]{2,1,0:T(8,128)(2,1)} custom-call(bf16[32,48,256]{2,1,0:T(8,128)(2,1)S(1)} %get-tuple-element.42.local, bf16[384,256]{1,0:T(8,128)(2,1)S(1)} %collective-permute-done.2.low, bf16[384,256]{1,0:T(8,128)(2,1)S(1)} %collective-permute-done.3.high, bf16[2304,256]{1,0:T(8,128)(2,1)S(1)} %copy-done.5), custom_call_target="tpu_custom_call" | custom-call | tf_op jit(solution)/shard_map/pallas_call | solution.py:245
  51.1 0.0 collective-permute-done.18.refs_1_
  51.1 0.0 collective-permute-done.19.refs_2_
  51.1 0.7 %shard_map.87 = f32[144,128]{1,0:T(8,128)} custom-call(f32[144,128]{1,0:T(8,128)S(1)} %get-tuple-element.63.own, bf16[144,128]{1,0:T(8,128)(2,1)S(1)} %collective-permute-done.17.refs_0_, bf16[144,128]{1,0:T(8,128)(2,1)S(1)} %collective-permute-done.18.refs_1_, bf16[144,128]{1,0:T(8,128)(2,1)S(1)} %collective-permute-done.19.refs_2_), custom_call_target="tpu_custom_call" | custom-call | tf_op jit(solution)/shard_map/pallas_call | solution.py:245
  51.7 0.0 collective-permute-done.12.refs_2_
  51.8 0.7 %shard_map.84 = f32[144,128]{1,0:T(8,128)} custom-call(f32[144,128]{1,0:T(8,128)S(1)} %get-tuple-element.53.own, bf16[144,128]{1,0:T(8,128)(2,1)S(1)} %collective-permute-done.10.refs_0_, bf16[144,128]{1,0:T(8,128)(2,1)S(1)} %collective-permute-done.11.refs_1_, bf16[144,128]{1,0:T(8,128)(2,1)S(1)} %collective-permute-done.12.refs_2_), custom_call_target="tpu_custom_call" | custom-call | tf_op jit(solution)/shard_map/pallas_call | solution.py:245
  (18 shorter events, 0.1 us)
Async XLA Ops:
  0.6 8.7 %copy-start = (bf16[1,32,48,256]{3,2,1,0:T(8,128)(2,1)S(1)}, bf16[1,32,48,256]{3,2,1,0:T(8,128)(2,1)}, u32[]{:S(2)}) copy-start(bf16[1,32,48,256]{3,2,1,0:T(8,128)(2,1)} %param.6) | copy-start | bytes 2359300
  0.6 1.2 %copy-start.1 = (bf16[1,32,48,256]{3,2,1,0:T(8,128)(2,1)S(1)}, bf16[1,32,48,256]{3,2,1,0:T(8,128)(2,1)}, u32[]{:S(2)}) copy-start(bf16[1,32,48,256]{3,2,1,0:T(8,128)(2,1)} %param.7) | copy-start | bytes 2359300
  1.8 7.4 %copy-start.2 = (bf16[1,32,48,256]{3,2,1,0:T(8,128)(2,1)S(1)}, bf16[1,32,48,256]{3,2,1,0:T(8,128)(2,1)}, u32[]{:S(2)}) copy-start(bf16[1,32,48,256]{3,2,1,0:T(8,128)(2,1)} %param.7) | copy-start | bytes 2359300
  1.9 11.3 %collective-permute-start = (bf16[576,256]{1,0:T(8,128)(2,1)S(1)}, bf16[576,256]{1,0:T(8,128)(2,1)S(1)}, u32[]{:S(2)}, u32[]{:S(2)}) collective-permute-start(bf16[576,256]{1,0:T(8,128)(2,1)S(1)} %get-tuple-element.35), channel_id=1, source_target_pairs={{0,4},{4,8},{8,12},{12,16},{16,20},{20,24},{24,28},{28,0},{1,5},{5... | collective-permute-start | bytes 884744 | tf_op jit(solution)/shard_map/ppermute | solution.py:265
  2.5 10.7 %collective-permute-start.1 = (bf16[576,256]{1,0:T(8,128)(2,1)S(1)}, bf16[576,256]{1,0:T(8,128)(2,1)S(1)}, u32[]{:S(2)}, u32[]{:S(2)}) collective-permute-start(bf16[576,256]{1,0:T(8,128)(2,1)S(1)} %get-tuple-element.36), channel_id=1, source_target_pairs={{0,28},{4,0},{8,4},{12,8},{16,12},{20,16},{24,20},{28,24},{1,29},{... | collective-permute-start | bytes 884744 | tf_op jit(solution)/shard_map/ppermute | solution.py:266
  5.4 1.1 %copy-start.3 = (bf16[1,32,48,256]{3,2,1,0:T(8,128)(2,1)S(1)}, bf16[1,32,48,256]{3,2,1,0:T(8,128)(2,1)}, u32[]{:S(2)}) copy-start(bf16[1,32,48,256]{3,2,1,0:T(8,128)(2,1)} %param.5) | copy-start | bytes 2359300
  6.6 9.4 %collective-permute-start.4 = (bf16[384,256]{1,0:T(8,128)(2,1)S(1)}, bf16[384,256]{1,0:T(8,128)(2,1)S(1)}, u32[]{:S(2)}, u32[]{:S(2)}) collective-permute-start(bf16[384,256]{1,0:T(8,128)(2,1)S(1)} %get-tuple-element.45), channel_id=1, source_target_pairs={{0,4},{4,8},{8,12},{12,16},{16,20},{20,24},{24,28},{28,0},{1,5},{5... | collective-permute-start | bytes 589832 | tf_op jit(solution)/shard_map/ppermute | solution.py:265
  6.6 9.4 %collective-permute-start.5 = (bf16[384,256]{1,0:T(8,128)(2,1)S(1)}, bf16[384,256]{1,0:T(8,128)(2,1)S(1)}, u32[]{:S(2)}, u32[]{:S(2)}) collective-permute-start(bf16[384,256]{1,0:T(8,128)(2,1)S(1)} %get-tuple-element.46), channel_id=1, source_target_pairs={{0,28},{4,0},{8,4},{12,8},{16,12},{20,16},{24,20},{28,24},{1,29},{... | collective-permute-start | bytes 589832 | tf_op jit(solution)/shard_map/ppermute | solution.py:266
  9.3 1.3 %copy-start.6 = (bf16[2304,256]{1,0:T(8,128)(2,1)S(1)}, bf16[2304,256]{1,0:T(8,128)(2,1)}, u32[]{:S(2)}) copy-start(bf16[2304,256]{1,0:T(8,128)(2,1)} %weight.2) | copy-start | bytes 3538948
  13.2 2.8 %copy-start.4 = (bf16[1,32,48,256]{3,2,1,0:T(8,128)(2,1)S(1)}, bf16[1,32,48,256]{3,2,1,0:T(8,128)(2,1)}, u32[]{:S(2)}) copy-start(bf16[1,32,48,256]{3,2,1,0:T(8,128)(2,1)} %param.5) | copy-start | bytes 2359300
  14.5 5.4 %collective-permute-start.13 = (bf16[2304,128]{1,0:T(8,128)(2,1)S(1)}, bf16[2304,128]{1,0:T(8,128)(2,1)S(1)}, u32[]{:S(2)}, u32[]{:S(2)}) collective-permute-start(bf16[2304,128]{1,0:T(8,128)(2,1)S(1)} %get-tuple-element.58), channel_id=1, source_target_pairs={{0,4},{4,0},{8,12},{12,8},{16,20},{20,16},{24,28},{28,24},{1,5},{5... | collective-permute-start | bytes 1769480 | tf_op jit(solution)/shard_map/ppermute | solution.py:279
  18.1 5.5 %collective-permute-start.6 = (bf16[2304,128]{1,0:T(8,128)(2,1)S(1)}, bf16[2304,128]{1,0:T(8,128)(2,1)S(1)}, u32[]{:S(2)}, u32[]{:S(2)}) collective-permute-start(bf16[2304,128]{1,0:T(8,128)(2,1)S(1)} %get-tuple-element.48), channel_id=1, source_target_pairs={{0,4},{4,0},{8,12},{12,8},{16,20},{20,16},{24,28},{28,24},{1,5},{5... | collective-permute-start | bytes 1769480 | tf_op jit(solution)/shard_map/ppermute | solution.py:279
  20.1 6.6 %collective-permute-start.14 = (bf16[576,128]{1,0:T(8,128)(2,1)S(1)}, bf16[576,128]{1,0:T(8,128)(2,1)S(1)}, u32[]{:S(2)}, u32[]{:S(2)}) collective-permute-start(bf16[576,128]{1,0:T(8,128)(2,1)S(1)} %get-tuple-element.60), channel_id=1, source_target_pairs={{0,8},{4,12},{8,0},{12,4},{16,24},{20,28},{24,16},{28,20},{1,9},{5... | collective-permute-start | bytes 442376 | tf_op jit(solution)/shard_map/ppermute | solution.py:282
  21.6 10.3 %collective-permute-start.15 = (bf16[576,128]{1,0:T(8,128)(2,1)S(1)}, bf16[576,128]{1,0:T(8,128)(2,1)S(1)}, u32[]{:S(2)}, u32[]{:S(2)}) collective-permute-start(bf16[576,128]{1,0:T(8,128)(2,1)S(1)} %get-tuple-element.61), channel_id=1, source_target_pairs={{0,16},{4,20},{8,24},{12,28},{16,0},{20,4},{24,8},{28,12},{1,17},{... | collective-permute-start | bytes 442376 | tf_op jit(solution)/shard_map/ppermute | solution.py:282
  22.1 9.9 %collective-permute-start.16 = (bf16[576,128]{1,0:T(8,128)(2,1)S(1)}, bf16[576,128]{1,0:T(8,128)(2,1)S(1)}, u32[]{:S(2)}, u32[]{:S(2)}) collective-permute-start(bf16[576,128]{1,0:T(8,128)(2,1)S(1)} %get-tuple-element.62), channel_id=1, source_target_pairs={{0,24},{4,28},{8,16},{12,20},{16,8},{20,12},{24,0},{28,4},{1,25},{... | collective-permute-start | bytes 442376 | tf_op jit(solution)/shard_map/ppermute | solution.py:282
  23.6 20.5 %collective-permute-start.2 = (bf16[384,256]{1,0:T(8,128)(2,1)S(1)}, bf16[384,256]{1,0:T(8,128)(2,1)S(1)}, u32[]{:S(2)}, u32[]{:S(2)}) collective-permute-start(bf16[384,256]{1,0:T(8,128)(2,1)S(1)} %get-tuple-element.43), channel_id=1, source_target_pairs={{0,4},{4,8},{8,12},{12,16},{16,20},{20,24},{24,28},{28,0},{1,5},{5... | collective-permute-start | bytes 589832 | tf_op jit(solution)/shard_map/ppermute | solution.py:265
  23.6 20.6 %collective-permute-start.3 = (bf16[384,256]{1,0:T(8,128)(2,1)S(1)}, bf16[384,256]{1,0:T(8,128)(2,1)S(1)}, u32[]{:S(2)}, u32[]{:S(2)}) collective-permute-start(bf16[384,256]{1,0:T(8,128)(2,1)S(1)} %get-tuple-element.44), channel_id=1, source_target_pairs={{0,28},{4,0},{8,4},{12,8},{16,12},{20,16},{24,20},{28,24},{1,29},{... | collective-permute-start | bytes 589832 | tf_op jit(solution)/shard_map/ppermute | solution.py:266
  26.3 22.3 %copy-start.5 = (bf16[2304,256]{1,0:T(8,128)(2,1)S(1)}, bf16[2304,256]{1,0:T(8,128)(2,1)}, u32[]{:S(2)}) copy-start(bf16[2304,256]{1,0:T(8,128)(2,1)} %weight.3) | copy-start | bytes 3538948
  26.7 10.6 %collective-permute-start.7 = (bf16[576,128]{1,0:T(8,128)(2,1)S(1)}, bf16[576,128]{1,0:T(8,128)(2,1)S(1)}, u32[]{:S(2)}, u32[]{:S(2)}) collective-permute-start(bf16[576,128]{1,0:T(8,128)(2,1)S(1)} %get-tuple-element.50), channel_id=1, source_target_pairs={{0,8},{4,12},{8,0},{12,4},{16,24},{20,28},{24,16},{28,20},{1,9},{5... | collective-permute-start | bytes 442376 | tf_op jit(solution)/shard_map/ppermute | solution.py:282
  31.9 6.9 %collective-permute-start.8 = (bf16[576,128]{1,0:T(8,128)(2,1)S(1)}, bf16[576,128]{1,0:T(8,128)(2,1)S(1)}, u32[]{:S(2)}, u32[]{:S(2)}) collective-permute-start(bf16[576,128]{1,0:T(8,128)(2,1)S(1)} %get-tuple-element.51), channel_id=1, source_target_pairs={{0,16},{4,20},{8,24},{12,28},{16,0},{20,4},{24,8},{28,12},{1,17},{... | collective-permute-start | bytes 442376 | tf_op jit(solution)/shard_map/ppermute | solution.py:282
  32.1 9.4 %collective-permute-start.9 = (bf16[576,128]{1,0:T(8,128)(2,1)S(1)}, bf16[576,128]{1,0:T(8,128)(2,1)S(1)}, u32[]{:S(2)}, u32[]{:S(2)}) collective-permute-start(bf16[576,128]{1,0:T(8,128)(2,1)S(1)} %get-tuple-element.52), channel_id=1, source_target_pairs={{0,24},{4,28},{8,16},{12,20},{16,8},{20,12},{24,0},{28,4},{1,25},{... | collective-permute-start | bytes 442376 | tf_op jit(solution)/shard_map/ppermute | solution.py:282
  37.2 8.8 %collective-permute-start.17 = (bf16[144,128]{1,0:T(8,128)(2,1)S(1)}, bf16[144,128]{1,0:T(8,128)(2,1)S(1)}, u32[]{:S(2)}, u32[]{:S(2)}) collective-permute-start(bf16[144,128]{1,0:T(8,128)(2,1)S(1)} %get-tuple-element.64), channel_id=1, source_target_pairs={{0,1},{1,0},{2,3},{3,2},{4,5},{5,4},{6,7},{7,6},{8,9},{9,8},{10,11... | collective-permute-start | bytes 110600 | tf_op jit(solution)/shard_map/ppermute | solution.py:290
  38.8 12.3 %collective-permute-start.18 = (bf16[144,128]{1,0:T(8,128)(2,1)S(1)}, bf16[144,128]{1,0:T(8,128)(2,1)S(1)}, u32[]{:S(2)}, u32[]{:S(2)}) collective-permute-start(bf16[144,128]{1,0:T(8,128)(2,1)S(1)} %get-tuple-element.65), channel_id=1, source_target_pairs={{0,2},{1,3},{2,0},{3,1},{4,6},{5,7},{6,4},{7,5},{8,10},{9,11},{10,... | collective-permute-start | bytes 110600 | tf_op jit(solution)/shard_map/ppermute | solution.py:290
  41.4 9.7 %collective-permute-start.19 = (bf16[144,128]{1,0:T(8,128)(2,1)S(1)}, bf16[144,128]{1,0:T(8,128)(2,1)S(1)}, u32[]{:S(2)}, u32[]{:S(2)}) collective-permute-start(bf16[144,128]{1,0:T(8,128)(2,1)S(1)} %get-tuple-element.66), channel_id=1, source_target_pairs={{0,3},{1,2},{2,1},{3,0},{4,7},{5,6},{6,5},{7,4},{8,11},{9,10},{10,... | collective-permute-start | bytes 110600 | tf_op jit(solution)/shard_map/ppermute | solution.py:290
  44.1 7.6 %collective-permute-start.10 = (bf16[144,128]{1,0:T(8,128)(2,1)S(1)}, bf16[144,128]{1,0:T(8,128)(2,1)S(1)}, u32[]{:S(2)}, u32[]{:S(2)}) collective-permute-start(bf16[144,128]{1,0:T(8,128)(2,1)S(1)} %get-tuple-element.54), channel_id=1, source_target_pairs={{0,1},{1,0},{2,3},{3,2},{4,5},{5,4},{6,7},{7,6},{8,9},{9,8},{10,11... | collective-permute-start | bytes 110600 | tf_op jit(solution)/shard_map/ppermute | solution.py:290
  44.2 7.6 %collective-permute-start.11 = (bf16[144,128]{1,0:T(8,128)(2,1)S(1)}, bf16[144,128]{1,0:T(8,128)(2,1)S(1)}, u32[]{:S(2)}, u32[]{:S(2)}) collective-permute-start(bf16[144,128]{1,0:T(8,128)(2,1)S(1)} %get-tuple-element.55), channel_id=1, source_target_pairs={{0,2},{1,3},{2,0},{3,1},{4,6},{5,7},{6,4},{7,5},{8,10},{9,11},{10,... | collective-permute-start | bytes 110600 | tf_op jit(solution)/shard_map/ppermute | solution.py:290
  46.0 5.8 %collective-permute-start.12 = (bf16[144,128]{1,0:T(8,128)(2,1)S(1)}, bf16[144,128]{1,0:T(8,128)(2,1)S(1)}, u32[]{:S(2)}, u32[]{:S(2)}) collective-permute-start(bf16[144,128]{1,0:T(8,128)(2,1)S(1)} %get-tuple-element.56), channel_id=1, source_target_pairs={{0,3},{1,2},{2,1},{3,0},{4,7},{5,6},{6,5},{7,4},{8,11},{9,10},{10,... | collective-permute-start | bytes 110600 | tf_op jit(solution)/shard_map/ppermute | solution.py:290
where the time goes:
time: 52.6 us; the launch traced here: 52.4 us
  starting transfers between devices  29 us (55%)
  Pallas kernels  10.4 us (20%)
  waiting for transfers between devices  8.63 us (16%)
  local copies, waits for them, and re-layouts  3.62 us (7%)
  between operations  0.77 us (1%)
    ppermute x6, starting transfers between devices, reduce_partials(): lax.ppermute(pieces[m - 1], 'dp', swap('dp', m))  11.2 us
    pallas_call x12, Pallas kernels, call(): pl.pallas_call(kernel, out_shape=[jax.ShapeDtypeStruct(s, t) for s, t in...  10.4 us
    ppermute x6, waiting for transfers between devices, reduce_partials(): lax.ppermute(paired[m], 'lon', swap('lon', 2 * m))  8.58 us
    ppermute x3, starting transfers between devices, exchange_edges(): high = lax.ppermute(low_edge, 'lon', ring('lon', -1))  8.21 us
    ppermute x6, starting transfers between devices, reduce_partials(): lax.ppermute(paired[m], 'lon', swap('lon', 2 * m))  5.7 us
    unnamed x14, local copies, waits for them, and re-layouts  3.62 us
    ppermute x2, starting transfers between devices, reduce_partials(): received = lax.ppermute(send, 'lon', swap('lon', 1))  3.31 us
  transfers between devices with their start and end apart: 20, of which 3 were waited for; matrix products, arithmetic and copies ran while one was open for 0% of the time, Pallas kernels for 18%

commit v1 on v0

--- a/solution.py
+++ b/solution.py
@@ -93,17 +93,25 @@
         gradient[at, :] = block[:, h * half : (h + 1) * half]
 
 
-def hand_out(gradient, keep, send, segments):
-    size = gradient.shape[0] // segments
+def hand_out(gradient, keep, send, segments, parts, split):
+    size = gradient.shape[0] // (segments * parts)
+    chips = segments // 2
     place = lax.axis_index("lon")
     core = lax.rem(place, 2)
     chip = place // 2
-    for m in range(segments // 2):
+    mine = lax.axis_index("dp")
+    if split:
+        order = [(m, n + low) for low in (0, 1) for m in range(chips) for n in range(0, parts, 2)]
+    else:
+        order = [(m, n) for m in range(chips) for n in range(parts)]
+    for slot, (m, n) in enumerate(order):
         pair = 2 * lax.bitwise_xor(chip, m)
-        mine = pl.ds(pl.multiple_of((pair + core) * size, size), size)
-        other = pl.ds(pl.multiple_of((pair + 1 - core) * size, size), size)
-        keep[m * size : (m + 1) * size, :] = gradient[mine, :].astype(BF16)
-        send[m * size : (m + 1) * size, :] = gradient[other, :].astype(BF16)
+        part = lax.bitwise_xor(mine, n)
+        to = pl.ds(slot * size, size)
+        own = pl.multiple_of(((pair + core) * parts + part) * size, size)
+        other = pl.multiple_of(((pair + 1 - core) * parts + part) * size, size)
+        keep[to, :] = gradient[pl.ds(own, size), :]
+        send[to, :] = gradient[pl.ds(other, size), :].astype(BF16)
 
 
 def second_early_kernel(pre, cot, weight, total, taps, low_still, high_still, turned, views, still):
@@ -126,7 +134,7 @@
 
 
 def second_late_kernel(
-    norm, segments, pre, low, high, early, taps, low_still, high_still, turned,
+    norm, segments, parts, pre, low, high, early, taps, low_still, high_still, turned,
     keep, send, local, edge_low, edge_high, low_views, high_views, low_total, high_total, gradient,
 ):
     rows, cols, chans = pre.shape
@@ -180,11 +188,11 @@
             if c in side:
                 block = block + side[c]
             place_tap(gradient, k, norm * block)
-    hand_out(gradient, keep, send, segments)
+    hand_out(gradient, keep, send, segments, parts, True)
 
 
 def first_weight_kernel(
-    norm, segments, inputs, low, high, local, keep, send, views, still, gradient
+    norm, segments, parts, inputs, low, high, local, keep, send, views, still, gradient
 ):
     rows, cols, chans = inputs.shape
     spread, pad = FIRST_SPREAD, FIRST_PAD
@@ -195,7 +203,7 @@
         for c in range(3):
             block = value[:, c * chans : (c + 1) * chans].T
             place_tap(gradient, 3 * r + c, block.astype(F32))
-    hand_out(gradient, keep, send, segments)
+    hand_out(gradient, keep, send, segments, parts, False)
 
 
 def first_input_kernel(local, low, high, weight, out, views, turned, total):
@@ -214,30 +222,16 @@
         high[p * width : (p + 1) * width, :] = row[cols - width :]
 
 
-def pair_kernel(keep, received, *outs):
-    size = outs[0].shape[0]
-    for m, out in enumerate(outs):
-        at = pl.ds(m * size, size)
-        out[...] = (keep[at, :].astype(F32) + received[at, :].astype(F32)).astype(BF16)
-
-
-def chip_kernel(count, *refs):
-    terms, own, pieces, level = refs[:count], refs[count], refs[count + 1 : -1], refs[-1]
-    level[...] = sum((t[...].astype(F32) for t in terms[1:]), terms[0][...].astype(F32))
-    size = own.shape[0]
-    me = lax.axis_index("dp")
-
-    def piece(m):
-        start = pl.multiple_of(lax.bitwise_xor(me, m) * size, size)
-        return level[pl.ds(start, size), :]
-
-    own[...] = piece(0)
-    for m, out in enumerate(pieces):
-        out[...] = piece(m + 1).astype(BF16)
-
-
-def last_kernel(own, *refs):
-    refs[-1][...] = sum((t[...].astype(F32) for t in refs[:-1]), own[...])
+def add_kernel(count, *refs):
+    terms, outs = refs[:count], refs[count:]
+    start = 0
+    for out in outs:
+        at = pl.ds(start, out.shape[0])
+        total = terms[0][at, :].astype(F32)
+        for term in terms[1:]:
+            total = total + term[at, :].astype(F32)
+        out[...] = total.astype(out.dtype)
+        start += out.shape[0]
 
 
 def call(kernel, outs, scratch, *operands, limit=20, flops=0):
@@ -272,33 +266,61 @@
     return call(functools.partial(edges_kernel, width), [(shape, BF16)] * 2, [], field, limit=4)
 
 
-def reduce_partials(keep, send):
-    chips = lax.axis_size("lon") // 2
-    parts = lax.axis_size("dp")
-    rows, lanes = keep.shape
-    received = lax.ppermute(send, "lon", swap("lon", 1))
-    piece = (rows // chips, lanes)
-    paired = call(pair_kernel, [(piece, BF16)] * chips, [], keep, received, limit=4)
-    arrived = [lax.ppermute(paired[m], "lon", swap("lon", 2 * m)) for m in range(1, chips)]
-    small = (piece[0] // parts, lanes)
-    own, *pieces = call(
-        functools.partial(chip_kernel, chips),
-        [(small, F32)] + [(small, BF16)] * (parts - 1),
-        [(piece, F32)],
-        paired[0], *arrived, limit=4,
-    )
-    arrived = [lax.ppermute(pieces[m - 1], "dp", swap("dp", m)) for m in range(1, parts)]
-    (total,) = call(last_kernel, [(small, F32)], [], own, *arrived, limit=4)
-    return total.reshape(-1)
+def add(terms, counts, parts_rows):
+    lanes = terms[0].shape[1]
+    outs = [((c * parts_rows, lanes), BF16 if i else F32) for i, c in enumerate(counts)]
+    kernel = functools.partial(add_kernel, len(terms))
+    return call(kernel, outs, [], *terms, limit=6)
+
+
+def move(axis, mask, value):
+    return lax.ppermute(value, axis, swap(axis, mask))
+
+
+def swaps(axis, masks, pieces):
+    got = [move(axis, mask, piece) for mask, piece in reversed(list(zip(masks, pieces)))]
+    return got[::-1]
+
+
+def chip_masks(count):
+    return range(2, count, 2)
+
+
+def reduce_first(keep, send):
+    segments, parts = lax.axis_size("lon"), lax.axis_size("dp")
+    chips = segments // 2
+    size = keep.shape[0] // (chips * parts)
+    received = move("lon", 1, send)
+    own, *others = add([keep, received], [parts] * chips, size)
+    others = swaps("lon", chip_masks(segments), others)
+    own, *others = add([own, *others], [1] * parts, size)
+    others = swaps("dp", range(1, parts), others)
+    (own,) = add([own, *others], [1], size)
+    return own.reshape(-1)
+
+
+def reduce_second(keep, send):
+    segments, parts = lax.axis_size("lon"), lax.axis_size("dp")
+    chips, half = segments // 2, parts // 2
+    size = keep.shape[0] // (chips * parts)
+    received = move("lon", 1, send)
+    own, other = add([keep, received], [chips * half] * 2, size)
+    received = move("dp", 1, other)
+    own, *others = add([own, received], [half] * chips, size)
+    others = swaps("lon", chip_masks(segments), others)
+    own, *others = add([own, *others], [1] * half, size)
+    others = swaps("dp", range(2, parts, 2), others)
+    (own,) = add([own, *others], [1], size)
+    return own.reshape(-1)
 
 
 def local(inputs, pre_act, cotangent, first_weight, second_weight):
     shape = inputs.shape
     inputs, pre_act, cotangent = (a.reshape(a.shape[1:]) for a in (inputs, pre_act, cotangent))
     rows, cols, chans = inputs.shape
-    segments = lax.axis_size("lon")
+    segments, parts = lax.axis_size("lon"), lax.axis_size("dp")
     cells = rows * cols
-    norm = float(shape[0] * cells * segments * lax.axis_size("dp")) ** -0.5
+    norm = float(shape[0] * cells * segments * parts) ** -0.5
     taps = first_weight.shape[0]
     cot_low, cot_high = exchange_edges(*edges_of(cotangent, SECOND_SPREAD))
     in_low, in_high = exchange_edges(*edges_of(inputs, FIRST_SPREAD))
@@ -321,15 +343,15 @@
     )
     strip = ((rows + 2 * SECOND_PAD) * cols // 2, chans)
     keep, send, local_grad, edge_low, edge_high = call(
-        functools.partial(second_late_kernel, norm, segments),
-        [(pieces, BF16), (pieces, BF16), ((rows, cols, chans), BF16), (edge, BF16), (edge, BF16)],
+        functools.partial(second_late_kernel, norm, segments, parts),
+        [(pieces, F32), (pieces, BF16), ((rows, cols, chans), BF16), (edge, BF16), (edge, BF16)],
         [(strip, BF16), (strip, BF16), (side, F32), (side, F32), (grid, F32)],
         pre_act, cot_low, cot_high, *early,
     )
-    second = reduce_partials(keep, send)
+    second = reduce_second(keep, send)
     keep, send = call(
-        functools.partial(first_weight_kernel, norm, segments),
-        [(pieces, BF16), (pieces, BF16)],
+        functools.partial(first_weight_kernel, norm, segments, parts),
+        [(pieces, F32), (pieces, BF16)],
         [
             (((rows + 2 * FIRST_PAD) * cols, 3 * chans), BF16),
             ((chans, cells), BF16),
@@ -337,7 +359,7 @@
         ],
         inputs, in_low, in_high, local_grad,
     )
-    first = reduce_partials(keep, send)
+    first = reduce_first(keep, send)
     grad_low, grad_high = exchange_edges(edge_low, edge_high)
     (input_gradient,) = call(
         first_input_kernel,

time: 52.6 us -> 55 us (1.046)
  waiting for transfers between devices: 8.63 us -> 15.9 us
  starting transfers between devices: 29 us -> 24.2 us
    ppermute x3, waiting for transfers between devices: 0.01 us -> 4.63 us  [exchange_edges(): low = lax.ppermute(high_edge, 'lon', ring('lon', 1))]
    ppermute x14 -> x13, starting transfers between devices: 20.2 us -> 17.6 us  [move(): return lax.ppermute(value, axis, swap(axis, mask))]
    ppermute x3, starting transfers between devices: 8.21 us -> 5.98 us  [exchange_edges(): high = lax.ppermute(low_edge, 'lon', ring('lon', -1))]
    ppermute x3, waiting for transfers between devices: 0.01 us -> 1.33 us  [exchange_edges(): high = lax.ppermute(low_edge, 'lon', ring('lon', -1))]
    ppermute x14 -> x13, waiting for transfers between devices: 8.61 us -> 9.92 us  [move(): return lax.ppermute(value, axis, swap(axis, mask))]
    pallas_call x12 -> x13, Pallas kernels: 10.4 us -> 10.3 us  [call(): pl.pallas_call(kernel, out_shape=[jax.ShapeDtypeStruct(s, t) for s, t in...]
    unnamed x14 -> x12, local copies, waits for them, and re-layouts: 3.62 us -> 3.62 us
  transfers between devices with their start and end apart: 20 -> 19, of which waited for: 3 -> 8; matrix products, arithmetic and copies ran while one was open for 0% -> 0% of each run, Pallas kernels for 18% -> 15%
where the time goes in v1:
time: 55 us; the launch traced here: 54.8 us
  starting transfers between devices  24.2 us (44%)
  waiting for transfers between devices  15.9 us (29%)
  Pallas kernels  10.3 us (19%)
  local copies, waits for them, and re-layouts  3.62 us (7%)
  between operations  0.77 us (1%)
    ppermute x13, starting transfers between devices, move(): return lax.ppermute(value, axis, swap(axis, mask))  17.6 us
    pallas_call x13, Pallas kernels, call(): pl.pallas_call(kernel, out_shape=[jax.ShapeDtypeStruct(s, t) for s, t in...  10.3 us
    ppermute x13, waiting for transfers between devices, move(): return lax.ppermute(value, axis, swap(axis, mask))  9.92 us
    ppermute x3, starting transfers between devices, exchange_edges(): high = lax.ppermute(low_edge, 'lon', ring('lon', -1))  5.98 us
    ppermute x3, waiting for transfers between devices, exchange_edges(): low = lax.ppermute(high_edge, 'lon', ring('lon', 1))  4.63 us
    unnamed x12, local copies, waits for them, and re-layouts  3.62 us
    ppermute x3, waiting for transfers between devices, exchange_edges(): high = lax.ppermute(low_edge, 'lon', ring('lon', -1))  1.33 us
  transfers between devices with their start and end apart: 19, of which 8 were waited for; matrix products, arithmetic and copies ran while one was open for 0% of the time, Pallas kernels for 15%

profile of v1, /device:TPU:0, one launch (start us, length us, event | category | flops | bytes accessed | tf_op | source)
XLA Modules:
  0.0 54.8 jit_solution(11666508620557698593)
XLA Ops:
  0.6 0.0 copy-start.1
  0.7 1.2 %copy-done.1 = bf16[1,32,48,256]{3,2,1,0:T(8,128)(2,1)S(1)} copy-done((bf16[1,32,48,256]{3,2,1,0:T(8,128)(2,1)S(1)}, bf16[1,32,48,256]{3,2,1,0:T(8,128)(2,1)}, u32[]{:S(2)}) %copy-start.1) | copy-done | bytes 786456
  1.8 0.1 shard_map.76
  1.9 0.5 collective-permute-start
  2.5 2.9 %collective-permute-start.1 = (bf16[576,256]{1,0:T(8,128)(2,1)S(1)}, bf16[576,256]{1,0:T(8,128)(2,1)S(1)}, u32[]{:S(2)}, u32[]{:S(2)}) collective-permute-start(bf16[576,256]{1,0:T(8,128)(2,1)S(1)} %get-tuple-element.36), channel_id=1, source_target_pairs={{0,28},{4,0},{8,4},{12,8},{16,12},{20,16},{24,20},{28,24},{1,29},{... | collective-permute-start | bytes 884744 | tf_op jit(solution)/shard_map/ppermute | solution.py:260
  5.4 1.1 %copy-done.2 = bf16[1,32,48,256]{3,2,1,0:T(8,128)(2,1)S(1)} copy-done((bf16[1,32,48,256]{3,2,1,0:T(8,128)(2,1)S(1)}, bf16[1,32,48,256]{3,2,1,0:T(8,128)(2,1)}, u32[]{:S(2)}) %copy-start.2) | copy-done | bytes 786456
  6.5 1.3 %copy-done.5 = bf16[2304,256]{1,0:T(8,128)(2,1)S(1)} copy-done((bf16[2304,256]{1,0:T(8,128)(2,1)S(1)}, bf16[2304,256]{1,0:T(8,128)(2,1)}, u32[]{:S(2)}) %copy-start.5) | copy-done | bytes 1179672
  7.8 2.6 %shard_map.77 = (f32[1536,256]{1,0:T(8,128)S(1)}, f32[2304,256]{1,0:T(8,128)S(1)}, bf16[256,768]{1,0:T(8,128)(2,1)S(1)}, bf16[256,768]{1,0:T(8,128)(2,1)S(1)}, bf16[2304,256]{1,0:T(8,128)(2,1)S(1)}) custom-call(bf16[32,48,256]{2,1,0:T(8,128)(2,1)S(1)} %bitcast.6, bf16[32,48,256]{2,1,0:T(8,128)(2,1)S(1)} %bitcast.9, bf16[2304,256]{1,0:T(8,128)(2,1)S(1)} %copy-done.5), custom_call_target="tpu_custom_call" | custom-call | tf_op jit(solution)/shard_map/pallas_call | solution.py:239
  10.4 0.0 collective-permute-done.low
  10.4 1.3 %collective-permute-done.1.high = bf16[576,256]{1,0:T(8,128)(2,1)S(1)} collective-permute-done((bf16[576,256]{1,0:T(8,128)(2,1)S(1)}, bf16[576,256]{1,0:T(8,128)(2,1)S(1)}, u32[]{:S(2)}, u32[]{:S(2)}) %collective-permute-start.1) | collective-permute-done | bytes 294944 | tf_op jit(solution)/shard_map/ppermute | solution.py:260
  11.8 1.3 %shard_map.78 = (f32[2304,128]{1,0:T(8,128)S(1)}, bf16[2304,128]{1,0:T(8,128)(2,1)S(1)}, bf16[32,48,256]{2,1,0:T(8,128)(2,1)S(1)}, bf16[384,256]{1,0:T(8,128)(2,1)S(1)}, bf16[384,256]{1,0:T(8,128)(2,1)S(1)}) custom-call(bf16[32,48,256]{2,1,0:T(8,128)(2,1)S(1)} %bitcast.7, bf16[576,256]{1,0:T(8,128)(2,1)S(1)} %collective-permute-done.low, ...), custom_call_target="tpu_custom_call" | custom-call | tf_op jit(solution)/shard_map/pallas_call | solution.py:239
  13.1 1.8 %collective-permute-start.13 = (bf16[2304,128]{1,0:T(8,128)(2,1)S(1)}, bf16[2304,128]{1,0:T(8,128)(2,1)S(1)}, u32[]{:S(2)}, u32[]{:S(2)}) collective-permute-start(bf16[2304,128]{1,0:T(8,128)(2,1)S(1)} %get-tuple-element.58), channel_id=1, source_target_pairs={{0,4},{4,0},{8,12},{12,8},{16,20},{20,16},{24,28},{28,24},{1,5},{5... | collective-permute-start | bytes 1769480 | tf_op jit(solution)/shard_map/ppermute | solution.py:277
  15.0 0.1 collective-permute-start.4
  15.0 2.6 %collective-permute-start.5 = (bf16[384,256]{1,0:T(8,128)(2,1)S(1)}, bf16[384,256]{1,0:T(8,128)(2,1)S(1)}, u32[]{:S(2)}, u32[]{:S(2)}) collective-permute-start(bf16[384,256]{1,0:T(8,128)(2,1)S(1)} %get-tuple-element.46), channel_id=1, source_target_pairs={{0,28},{4,0},{8,4},{12,8},{16,12},{20,16},{24,20},{28,24},{1,29},{... | collective-permute-start | bytes 589832 | tf_op jit(solution)/shard_map/ppermute | solution.py:260
  17.7 4.6 %collective-permute-done.4.low = bf16[384,256]{1,0:T(8,128)(2,1)S(1)} collective-permute-done((bf16[384,256]{1,0:T(8,128)(2,1)S(1)}, bf16[384,256]{1,0:T(8,128)(2,1)S(1)}, u32[]{:S(2)}, u32[]{:S(2)}) %collective-permute-start.4) | collective-permute-done | bytes 196640 | tf_op jit(solution)/shard_map/ppermute | solution.py:259
  22.3 0.0 collective-permute-done.5.high
  22.3 2.1 %shard_map.81 = (f32[2304,128]{1,0:T(8,128)S(1)}, bf16[2304,128]{1,0:T(8,128)(2,1)S(1)}) custom-call(bf16[32,48,256]{2,1,0:T(8,128)(2,1)S(1)} %bitcast.11, bf16[384,256]{1,0:T(8,128)(2,1)S(1)} %collective-permute-done.4.low, bf16[384,256]{1,0:T(8,128)(2,1)S(1)} %collective-permute-done.5.high, bf16[32,48,256]{2,1,0:T(8,128)(2,1)S(1)} %get-tuple-element.42.local), custom_call_target="tpu_custom_call" | custom-call | tf_op jit(solution)/shard_map/pallas_call | solution.py:239
  24.4 0.2 collective-permute-start.6
  24.6 0.1 shard_map.85
  24.7 1.6 %collective-permute-start.14 = (bf16[1152,128]{1,0:T(8,128)(2,1)S(1)}, bf16[1152,128]{1,0:T(8,128)(2,1)S(1)}, u32[]{:S(2)}, u32[]{:S(2)}) collective-permute-start(bf16[1152,128]{1,0:T(8,128)(2,1)S(1)} %get-tuple-element.60), channel_id=1, source_target_pairs={{0,1},{1,0},{2,3},{3,2},{4,5},{5,4},{6,7},{7,6},{8,9},{9,8},{10,11... | collective-permute-start | bytes 884744 | tf_op jit(solution)/shard_map/ppermute | solution.py:277
  26.3 0.1 collective-permute-done.6.refs_1_
  26.5 0.1 shard_map.82
  26.6 0.0 copy-start.4
  26.6 1.0 %collective-permute-start.7 = (bf16[576,128]{1,0:T(8,128)(2,1)S(1)}, bf16[576,128]{1,0:T(8,128)(2,1)S(1)}, u32[]{:S(2)}, u32[]{:S(2)}) collective-permute-start(bf16[576,128]{1,0:T(8,128)(2,1)S(1)} %get-tuple-element.50), channel_id=1, source_target_pairs={{0,8},{4,12},{8,0},{12,4},{16,24},{20,28},{24,16},{28,20},{1,9},{5... | collective-permute-start | bytes 442376 | tf_op jit(solution)/shard_map/ppermute | solution.py:277
  27.6 1.5 %collective-permute-start.8 = (bf16[576,128]{1,0:T(8,128)(2,1)S(1)}, bf16[576,128]{1,0:T(8,128)(2,1)S(1)}, u32[]{:S(2)}, u32[]{:S(2)}) collective-permute-start(bf16[576,128]{1,0:T(8,128)(2,1)S(1)} %get-tuple-element.51), channel_id=1, source_target_pairs={{0,16},{4,20},{8,24},{12,28},{16,0},{20,4},{24,8},{28,12},{1,17},{... | collective-permute-start | bytes 442376 | tf_op jit(solution)/shard_map/ppermute | solution.py:277
  29.1 1.0 %collective-permute-start.9 = (bf16[576,128]{1,0:T(8,128)(2,1)S(1)}, bf16[576,128]{1,0:T(8,128)(2,1)S(1)}, u32[]{:S(2)}, u32[]{:S(2)}) collective-permute-start(bf16[576,128]{1,0:T(8,128)(2,1)S(1)} %get-tuple-element.52), channel_id=1, source_target_pairs={{0,24},{4,28},{8,16},{12,20},{16,8},{20,12},{24,0},{28,4},{1,25},{... | collective-permute-start | bytes 442376 | tf_op jit(solution)/shard_map/ppermute | solution.py:277
  30.1 0.0 collective-permute-start.2
  30.1 3.9 %collective-permute-done.14.refs_1_ = bf16[1152,128]{1,0:T(8,128)(2,1)S(1)} collective-permute-done((bf16[1152,128]{1,0:T(8,128)(2,1)S(1)}, bf16[1152,128]{1,0:T(8,128)(2,1)S(1)}, u32[]{:S(2)}, u32[]{:S(2)}) %collective-permute-start.14) | collective-permute-done | bytes 294944 | tf_op jit(solution)/shard_map/ppermute | solution.py:277
  34.0 0.4 collective-permute-start.3
  34.5 0.1 shard_map.86
  34.6 0.8 %collective-permute-start.15 = (bf16[288,128]{1,0:T(8,128)(2,1)S(1)}, bf16[288,128]{1,0:T(8,128)(2,1)S(1)}, u32[]{:S(2)}, u32[]{:S(2)}) collective-permute-start(bf16[288,128]{1,0:T(8,128)(2,1)S(1)} %get-tuple-element.62), channel_id=1, source_target_pairs={{0,8},{4,12},{8,0},{12,4},{16,24},{20,28},{24,16},{28,20},{1,9},{5... | collective-permute-start | bytes 221192 | tf_op jit(solution)/shard_map/ppermute | solution.py:277
  35.4 2.3 %collective-permute-done.8.refs_2_ = bf16[576,128]{1,0:T(8,128)(2,1)S(1)} collective-permute-done((bf16[576,128]{1,0:T(8,128)(2,1)S(1)}, bf16[576,128]{1,0:T(8,128)(2,1)S(1)}, u32[]{:S(2)}, u32[]{:S(2)}) %collective-permute-start.8) | collective-permute-done | bytes 147488 | tf_op jit(solution)/shard_map/ppermute | solution.py:277
  37.7 2.7 %collective-permute-start.16 = (bf16[288,128]{1,0:T(8,128)(2,1)S(1)}, bf16[288,128]{1,0:T(8,128)(2,1)S(1)}, u32[]{:S(2)}, u32[]{:S(2)}) collective-permute-start(bf16[288,128]{1,0:T(8,128)(2,1)S(1)} %get-tuple-element.63), channel_id=1, source_target_pairs={{0,16},{4,20},{8,24},{12,28},{16,0},{20,4},{24,8},{28,12},{1,17},{... | collective-permute-start | bytes 221192 | tf_op jit(solution)/shard_map/ppermute | solution.py:277
  40.3 0.0 collective-permute-done.9.refs_3_
  40.3 0.0 collective-permute-start.17
  40.3 0.1 shard_map.83
  40.4 1.9 %collective-permute-done.15.refs_1_ = bf16[288,128]{1,0:T(8,128)(2,1)S(1)} collective-permute-done((bf16[288,128]{1,0:T(8,128)(2,1)S(1)}, bf16[288,128]{1,0:T(8,128)(2,1)S(1)}, u32[]{:S(2)}, u32[]{:S(2)}) %collective-permute-start.15) | collective-permute-done | bytes 73760 | tf_op jit(solution)/shard_map/ppermute | solution.py:277
  42.3 1.6 %collective-permute-start.10 = (bf16[144,128]{1,0:T(8,128)(2,1)S(1)}, bf16[144,128]{1,0:T(8,128)(2,1)S(1)}, u32[]{:S(2)}, u32[]{:S(2)}) collective-permute-start(bf16[144,128]{1,0:T(8,128)(2,1)S(1)} %get-tuple-element.54), channel_id=1, source_target_pairs={{0,1},{1,0},{2,3},{3,2},{4,5},{5,4},{6,7},{7,6},{8,9},{9,8},{10,11... | collective-permute-start | bytes 110600 | tf_op jit(solution)/shard_map/ppermute | solution.py:277
  43.9 2.6 %collective-permute-start.11 = (bf16[144,128]{1,0:T(8,128)(2,1)S(1)}, bf16[144,128]{1,0:T(8,128)(2,1)S(1)}, u32[]{:S(2)}, u32[]{:S(2)}) collective-permute-start(bf16[144,128]{1,0:T(8,128)(2,1)S(1)} %get-tuple-element.55), channel_id=1, source_target_pairs={{0,2},{1,3},{2,0},{3,1},{4,6},{5,7},{6,4},{7,5},{8,10},{9,11},{10,... | collective-permute-start | bytes 110600 | tf_op jit(solution)/shard_map/ppermute | solution.py:277
  46.5 2.7 %collective-permute-start.12 = (bf16[144,128]{1,0:T(8,128)(2,1)S(1)}, bf16[144,128]{1,0:T(8,128)(2,1)S(1)}, u32[]{:S(2)}, u32[]{:S(2)}) collective-permute-start(bf16[144,128]{1,0:T(8,128)(2,1)S(1)} %get-tuple-element.56), channel_id=1, source_target_pairs={{0,3},{1,2},{2,1},{3,0},{4,7},{5,6},{6,5},{7,4},{8,11},{9,10},{10,... | collective-permute-start | bytes 110600 | tf_op jit(solution)/shard_map/ppermute | solution.py:277
  49.2 0.1 collective-permute-start.18
  49.3 0.0 collective-permute-done.3.high
  49.3 2.5 %shard_map.79 = bf16[32,48,256]{2,1,0:T(8,128)(2,1)} custom-call(bf16[32,48,256]{2,1,0:T(8,128)(2,1)S(1)} %get-tuple-element.42.local, bf16[384,256]{1,0:T(8,128)(2,1)S(1)} %collective-permute-done.2.low, bf16[384,256]{1,0:T(8,128)(2,1)S(1)} %collective-permute-done.3.high, bf16[2304,256]{1,0:T(8,128)(2,1)S(1)} %copy-done.4), custom_call_target="tpu_custom_call" | custom-call | tf_op jit(solution)/shard_map/pallas_call | solution.py:239
  51.9 0.0 collective-permute-done.10.refs_1_
  51.9 0.4 collective-permute-done.12.refs_3_
  52.2 0.7 %shard_map.84 = f32[144,128]{1,0:T(8,128)} custom-call(f32[144,128]{1,0:T(8,128)S(1)} %get-tuple-element.53.refs_0_, bf16[144,128]{1,0:T(8,128)(2,1)S(1)} %collective-permute-done.10.refs_1_, bf16[144,128]{1,0:T(8,128)(2,1)S(1)} %collective-permute-done.11.refs_2_, bf16[144,128]{1,0:T(8,128)(2,1)S(1)} %collective-permute-done.12.refs_3_), custom_call_target="tpu_custom_call" | custom-call | tf_op jit(solution)/shard_map/pallas_call | solution.py:239
  52.9 1.3 %collective-permute-done.18.refs_1_ = bf16[144,128]{1,0:T(8,128)(2,1)S(1)} collective-permute-done((bf16[144,128]{1,0:T(8,128)(2,1)S(1)}, bf16[144,128]{1,0:T(8,128)(2,1)S(1)}, u32[]{:S(2)}, u32[]{:S(2)}) %collective-permute-start.18) | collective-permute-done | bytes 36896 | tf_op jit(solution)/shard_map/ppermute | solution.py:277
  54.2 0.6 %shard_map.88 = f32[144,128]{1,0:T(8,128)} custom-call(f32[144,128]{1,0:T(8,128)S(1)} %get-tuple-element.65.refs_0_, bf16[144,128]{1,0:T(8,128)(2,1)S(1)} %collective-permute-done.18.refs_1_), custom_call_target="tpu_custom_call" | custom-call | tf_op jit(solution)/shard_map/pallas_call | solution.py:239
  (15 shorter events, 0.1 us)
Async XLA Ops:
  0.6 4.8 %copy-start = (bf16[1,32,48,256]{3,2,1,0:T(8,128)(2,1)S(1)}, bf16[1,32,48,256]{3,2,1,0:T(8,128)(2,1)}, u32[]{:S(2)}) copy-start(bf16[1,32,48,256]{3,2,1,0:T(8,128)(2,1)} %param.6) | copy-start | bytes 2359300
  0.6 1.2 %copy-start.1 = (bf16[1,32,48,256]{3,2,1,0:T(8,128)(2,1)S(1)}, bf16[1,32,48,256]{3,2,1,0:T(8,128)(2,1)}, u32[]{:S(2)}) copy-start(bf16[1,32,48,256]{3,2,1,0:T(8,128)(2,1)} %param.7) | copy-start | bytes 2359300
  1.9 8.5 %collective-permute-start = (bf16[576,256]{1,0:T(8,128)(2,1)S(1)}, bf16[576,256]{1,0:T(8,128)(2,1)S(1)}, u32[]{:S(2)}, u32[]{:S(2)}) collective-permute-start(bf16[576,256]{1,0:T(8,128)(2,1)S(1)} %get-tuple-element.35), channel_id=1, source_target_pairs={{0,4},{4,8},{8,12},{12,16},{16,20},{20,24},{24,28},{28,0},{1,5},{5... | collective-permute-start | bytes 884744 | tf_op jit(solution)/shard_map/ppermute | solution.py:259
  2.5 9.3 %collective-permute-start.1 = (bf16[576,256]{1,0:T(8,128)(2,1)S(1)}, bf16[576,256]{1,0:T(8,128)(2,1)S(1)}, u32[]{:S(2)}, u32[]{:S(2)}) collective-permute-start(bf16[576,256]{1,0:T(8,128)(2,1)S(1)} %get-tuple-element.36), channel_id=1, source_target_pairs={{0,28},{4,0},{8,4},{12,8},{16,12},{20,16},{24,20},{28,24},{1,29},{... | collective-permute-start | bytes 884744 | tf_op jit(solution)/shard_map/ppermute | solution.py:260
  5.4 1.1 %copy-start.2 = (bf16[1,32,48,256]{3,2,1,0:T(8,128)(2,1)S(1)}, bf16[1,32,48,256]{3,2,1,0:T(8,128)(2,1)}, u32[]{:S(2)}) copy-start(bf16[1,32,48,256]{3,2,1,0:T(8,128)(2,1)} %param.7) | copy-start | bytes 2359300
  6.5 1.3 %copy-start.5 = (bf16[2304,256]{1,0:T(8,128)(2,1)S(1)}, bf16[2304,256]{1,0:T(8,128)(2,1)}, u32[]{:S(2)}) copy-start(bf16[2304,256]{1,0:T(8,128)(2,1)} %weight.2) | copy-start | bytes 3538948
  11.8 3.1 %copy-start.3 = (bf16[1,32,48,256]{3,2,1,0:T(8,128)(2,1)S(1)}, bf16[1,32,48,256]{3,2,1,0:T(8,128)(2,1)}, u32[]{:S(2)}) copy-start(bf16[1,32,48,256]{3,2,1,0:T(8,128)(2,1)} %param.5) | copy-start | bytes 2359300
  13.1 11.5 %collective-permute-start.13 = (bf16[2304,128]{1,0:T(8,128)(2,1)S(1)}, bf16[2304,128]{1,0:T(8,128)(2,1)S(1)}, u32[]{:S(2)}, u32[]{:S(2)}) collective-permute-start(bf16[2304,128]{1,0:T(8,128)(2,1)S(1)} %get-tuple-element.58), channel_id=1, source_target_pairs={{0,4},{4,0},{8,12},{12,8},{16,20},{20,16},{24,28},{28,24},{1,5},{5... | collective-permute-start | bytes 1769480 | tf_op jit(solution)/shard_map/ppermute | solution.py:277
  15.0 7.3 %collective-permute-start.4 = (bf16[384,256]{1,0:T(8,128)(2,1)S(1)}, bf16[384,256]{1,0:T(8,128)(2,1)S(1)}, u32[]{:S(2)}, u32[]{:S(2)}) collective-permute-start(bf16[384,256]{1,0:T(8,128)(2,1)S(1)} %get-tuple-element.45), channel_id=1, source_target_pairs={{0,4},{4,8},{8,12},{12,16},{16,20},{20,24},{24,28},{28,0},{1,5},{5... | collective-permute-start | bytes 589832 | tf_op jit(solution)/shard_map/ppermute | solution.py:259
  15.0 7.2 %collective-permute-start.5 = (bf16[384,256]{1,0:T(8,128)(2,1)S(1)}, bf16[384,256]{1,0:T(8,128)(2,1)S(1)}, u32[]{:S(2)}, u32[]{:S(2)}) collective-permute-start(bf16[384,256]{1,0:T(8,128)(2,1)S(1)} %get-tuple-element.46), channel_id=1, source_target_pairs={{0,28},{4,0},{8,4},{12,8},{16,12},{20,16},{24,20},{28,24},{1,29},{... | collective-permute-start | bytes 589832 | tf_op jit(solution)/shard_map/ppermute | solution.py:260
  24.4 2.1 %collective-permute-start.6 = (bf16[2304,128]{1,0:T(8,128)(2,1)S(1)}, bf16[2304,128]{1,0:T(8,128)(2,1)S(1)}, u32[]{:S(2)}, u32[]{:S(2)}) collective-permute-start(bf16[2304,128]{1,0:T(8,128)(2,1)S(1)} %get-tuple-element.48), channel_id=1, source_target_pairs={{0,4},{4,0},{8,12},{12,8},{16,20},{20,16},{24,28},{28,24},{1,5},{5... | collective-permute-start | bytes 1769480 | tf_op jit(solution)/shard_map/ppermute | solution.py:277
  24.7 9.4 %collective-permute-start.14 = (bf16[1152,128]{1,0:T(8,128)(2,1)S(1)}, bf16[1152,128]{1,0:T(8,128)(2,1)S(1)}, u32[]{:S(2)}, u32[]{:S(2)}) collective-permute-start(bf16[1152,128]{1,0:T(8,128)(2,1)S(1)} %get-tuple-element.60), channel_id=1, source_target_pairs={{0,1},{1,0},{2,3},{3,2},{4,5},{5,4},{6,7},{7,6},{8,9},{9,8},{10,11... | collective-permute-start | bytes 884744 | tf_op jit(solution)/shard_map/ppermute | solution.py:277
  26.6 22.8 %copy-start.4 = (bf16[2304,256]{1,0:T(8,128)(2,1)S(1)}, bf16[2304,256]{1,0:T(8,128)(2,1)}, u32[]{:S(2)}) copy-start(bf16[2304,256]{1,0:T(8,128)(2,1)} %weight.3) | copy-start | bytes 3538948
  26.6 8.0 %collective-permute-start.7 = (bf16[576,128]{1,0:T(8,128)(2,1)S(1)}, bf16[576,128]{1,0:T(8,128)(2,1)S(1)}, u32[]{:S(2)}, u32[]{:S(2)}) collective-permute-start(bf16[576,128]{1,0:T(8,128)(2,1)S(1)} %get-tuple-element.50), channel_id=1, source_target_pairs={{0,8},{4,12},{8,0},{12,4},{16,24},{20,28},{24,16},{28,20},{1,9},{5... | collective-permute-start | bytes 442376 | tf_op jit(solution)/shard_map/ppermute | solution.py:277
  27.6 10.1 %collective-permute-start.8 = (bf16[576,128]{1,0:T(8,128)(2,1)S(1)}, bf16[576,128]{1,0:T(8,128)(2,1)S(1)}, u32[]{:S(2)}, u32[]{:S(2)}) collective-permute-start(bf16[576,128]{1,0:T(8,128)(2,1)S(1)} %get-tuple-element.51), channel_id=1, source_target_pairs={{0,16},{4,20},{8,24},{12,28},{16,0},{20,4},{24,8},{28,12},{1,17},{... | collective-permute-start | bytes 442376 | tf_op jit(solution)/shard_map/ppermute | solution.py:277
  29.1 11.2 %collective-permute-start.9 = (bf16[576,128]{1,0:T(8,128)(2,1)S(1)}, bf16[576,128]{1,0:T(8,128)(2,1)S(1)}, u32[]{:S(2)}, u32[]{:S(2)}) collective-permute-start(bf16[576,128]{1,0:T(8,128)(2,1)S(1)} %get-tuple-element.52), channel_id=1, source_target_pairs={{0,24},{4,28},{8,16},{12,20},{16,8},{20,12},{24,0},{28,4},{1,25},{... | collective-permute-start | bytes 442376 | tf_op jit(solution)/shard_map/ppermute | solution.py:277
  30.1 19.1 %collective-permute-start.2 = (bf16[384,256]{1,0:T(8,128)(2,1)S(1)}, bf16[384,256]{1,0:T(8,128)(2,1)S(1)}, u32[]{:S(2)}, u32[]{:S(2)}) collective-permute-start(bf16[384,256]{1,0:T(8,128)(2,1)S(1)} %get-tuple-element.43), channel_id=1, source_target_pairs={{0,4},{4,8},{8,12},{12,16},{16,20},{20,24},{24,28},{28,0},{1,5},{5... | collective-permute-start | bytes 589832 | tf_op jit(solution)/shard_map/ppermute | solution.py:259
  34.0 15.3 %collective-permute-start.3 = (bf16[384,256]{1,0:T(8,128)(2,1)S(1)}, bf16[384,256]{1,0:T(8,128)(2,1)S(1)}, u32[]{:S(2)}, u32[]{:S(2)}) collective-permute-start(bf16[384,256]{1,0:T(8,128)(2,1)S(1)} %get-tuple-element.44), channel_id=1, source_target_pairs={{0,28},{4,0},{8,4},{12,8},{16,12},{20,16},{24,20},{28,24},{1,29},{... | collective-permute-start | bytes 589832 | tf_op jit(solution)/shard_map/ppermute | solution.py:260
  34.6 7.8 %collective-permute-start.15 = (bf16[288,128]{1,0:T(8,128)(2,1)S(1)}, bf16[288,128]{1,0:T(8,128)(2,1)S(1)}, u32[]{:S(2)}, u32[]{:S(2)}) collective-permute-start(bf16[288,128]{1,0:T(8,128)(2,1)S(1)} %get-tuple-element.62), channel_id=1, source_target_pairs={{0,8},{4,12},{8,0},{12,4},{16,24},{20,28},{24,16},{28,20},{1,9},{5... | collective-permute-start | bytes 221192 | tf_op jit(solution)/shard_map/ppermute | solution.py:277
  37.7 6.2 %collective-permute-start.16 = (bf16[288,128]{1,0:T(8,128)(2,1)S(1)}, bf16[288,128]{1,0:T(8,128)(2,1)S(1)}, u32[]{:S(2)}, u32[]{:S(2)}) collective-permute-start(bf16[288,128]{1,0:T(8,128)(2,1)S(1)} %get-tuple-element.63), channel_id=1, source_target_pairs={{0,16},{4,20},{8,24},{12,28},{16,0},{20,4},{24,8},{28,12},{1,17},{... | collective-permute-start | bytes 221192 | tf_op jit(solution)/shard_map/ppermute | solution.py:277
  40.3 6.2 %collective-permute-start.17 = (bf16[288,128]{1,0:T(8,128)(2,1)S(1)}, bf16[288,128]{1,0:T(8,128)(2,1)S(1)}, u32[]{:S(2)}, u32[]{:S(2)}) collective-permute-start(bf16[288,128]{1,0:T(8,128)(2,1)S(1)} %get-tuple-element.64), channel_id=1, source_target_pairs={{0,24},{4,28},{8,16},{12,20},{16,8},{20,12},{24,0},{28,4},{1,25},{... | collective-permute-start | bytes 221192 | tf_op jit(solution)/shard_map/ppermute | solution.py:277
  42.3 9.5 %collective-permute-start.10 = (bf16[144,128]{1,0:T(8,128)(2,1)S(1)}, bf16[144,128]{1,0:T(8,128)(2,1)S(1)}, u32[]{:S(2)}, u32[]{:S(2)}) collective-permute-start(bf16[144,128]{1,0:T(8,128)(2,1)S(1)} %get-tuple-element.54), channel_id=1, source_target_pairs={{0,1},{1,0},{2,3},{3,2},{4,5},{5,4},{6,7},{7,6},{8,9},{9,8},{10,11... | collective-permute-start | bytes 110600 | tf_op jit(solution)/shard_map/ppermute | solution.py:277
  43.9 8.0 %collective-permute-start.11 = (bf16[144,128]{1,0:T(8,128)(2,1)S(1)}, bf16[144,128]{1,0:T(8,128)(2,1)S(1)}, u32[]{:S(2)}, u32[]{:S(2)}) collective-permute-start(bf16[144,128]{1,0:T(8,128)(2,1)S(1)} %get-tuple-element.55), channel_id=1, source_target_pairs={{0,2},{1,3},{2,0},{3,1},{4,6},{5,7},{6,4},{7,5},{8,10},{9,11},{10,... | collective-permute-start | bytes 110600 | tf_op jit(solution)/shard_map/ppermute | solution.py:277
  46.5 5.8 %collective-permute-start.12 = (bf16[144,128]{1,0:T(8,128)(2,1)S(1)}, bf16[144,128]{1,0:T(8,128)(2,1)S(1)}, u32[]{:S(2)}, u32[]{:S(2)}) collective-permute-start(bf16[144,128]{1,0:T(8,128)(2,1)S(1)} %get-tuple-element.56), channel_id=1, source_target_pairs={{0,3},{1,2},{2,1},{3,0},{4,7},{5,6},{6,5},{7,4},{8,11},{9,10},{10,... | collective-permute-start | bytes 110600 | tf_op jit(solution)/shard_map/ppermute | solution.py:277
  49.2 4.9 %collective-permute-start.18 = (bf16[144,128]{1,0:T(8,128)(2,1)S(1)}, bf16[144,128]{1,0:T(8,128)(2,1)S(1)}, u32[]{:S(2)}, u32[]{:S(2)}) collective-permute-start(bf16[144,128]{1,0:T(8,128)(2,1)S(1)} %get-tuple-element.66), channel_id=1, source_target_pairs={{0,2},{1,3},{2,0},{3,1},{4,6},{5,7},{6,4},{7,5},{8,10},{9,11},{10,... | collective-permute-start | bytes 110600 | tf_op jit(solution)/shard_map/ppermute | solution.py:277
